TPU v7x, 32 devices: a whole 2x2x4 slice. The times are simulated.
32 devices in a mesh: fsdp: 16 (over z, y, core), tp: 2 (over x).
Axes of the slice: x: 2, y: 2, z: 4, core: 2. Of those that a mesh axis runs over, the one named last changes fastest.
Arguments:
- hidden: bfloat16 [32, 5120], P(None, 'fsdp'), may hold values from -20 to 20
- query_weight: bfloat16 [5120, 5120], P(None, ('tp', 'fsdp')), may hold values from -0.078125 to 0.078125
- key_weight: bfloat16 [5120, 1024], P(None, ('tp', 'fsdp')), may hold values from -0.078125 to 0.078125
- value_weight: bfloat16 [5120, 1024], P(None, ('tp', 'fsdp')), may hold values from -0.078125 to 0.078125
- output_weight: bfloat16 [5120, 5120], P(('tp', 'fsdp')), may hold values from -0.078125 to 0.078125
- gate_weight: bfloat16 [5120, 27648], P(None, ('tp', 'fsdp')), may hold values from -0.078125 to 0.078125
- up_weight: bfloat16 [5120, 27648], P(None, ('tp', 'fsdp')), may hold values from -0.078125 to 0.078125
- down_weight: bfloat16 [27648, 5120], P(('tp', 'fsdp')), may hold values from -0.0390625 to 0.0390625
- history: float32 [7, 1024], replicated, may hold values from 0.0001 to 1, as said below
- slot: int32 [1], replicated, may hold values from 0 to 1023
- lengths: int32 [32], P('fsdp'), may hold values from 512 to 4096, as said below
- key_cache: bfloat16 [32, 4096, 1024], P('fsdp', None, 'tp'), may hold values from -1000 to 1000
- value_cache: bfloat16 [32, 4096, 1024], P('fsdp', None, 'tp'), may hold values from -6 to 6
Outputs:
- attention_out: bfloat16 [32, 5120], P('fsdp', 'tp')
- query_rollout: bfloat16 [5120, 5120], P('fsdp', 'tp')
- key_rollout: bfloat16 [5120, 1024], P('fsdp', 'tp')
- value_rollout: bfloat16 [5120, 1024], P('fsdp', 'tp')
- output_rollout: bfloat16 [5120, 5120], P('tp', 'fsdp')
- gate_rollout: bfloat16 [5120, 27648], P('fsdp', 'tp')
- up_rollout: bfloat16 [5120, 27648], P('fsdp', 'tp')
- down_rollout: bfloat16 [27648, 5120], P('tp', 'fsdp')
- new_history: float32 [7, 1024], replicated
Inputs may be any that keep to these rules, and one draw needn't show every extreme that they name: `history`: strictly positive. `lengths`: some sequence has all 4096 slots valid.
All inputs are finite; a program needn't handle non-finite values.
Results may differ from a plain program's by a relative error of at most 0.012.
The roundings to bfloat16 on the way count: a program that leaves them out, or rounds other values in their place, can miss the bound.
Values may be sent and summed in bfloat16 or wider, within the bound.
A program may use at most 192 MiB of HBM per device.

v0:
```python
import jax
import jax.numpy as jnp
from jax import lax
from jax.sharding import PartitionSpec as P

D = 5120
HEADS = 40
KV_HEADS = 8
HEAD_DIM = 128
target_peak = 4.0
norm_eps = 1e-06
rope_theta = 1000000.0


def largest(tensor):
    return jnp.max(jnp.abs(tensor.astype(jnp.float32)))


def scaling(peaks, history, slot):
    marked = lax.broadcasted_iota(jnp.int32, history.shape, 1) == slot[0]
    kept = jnp.max(jnp.where(marked, jnp.zeros_like(history), history), axis=1)
    return (target_peak / jnp.maximum(peaks, kept), jnp.where(marked, peaks[:, None], history))


def quantize(tensor, factor):
    return (tensor.astype(jnp.float32) * factor).astype(jnp.bfloat16)


def rotate(vectors, positions):
    half_dim = vectors.shape[-1] // 2
    ladder = jnp.arange(half_dim, dtype=jnp.float32)
    spread = rope_theta ** (-2.0 * ladder / vectors.shape[-1])
    angle = positions.astype(jnp.float32)[:, None] * spread[None, :]
    cosine = jnp.cos(angle)[:, None, :]
    sine = jnp.sin(angle)[:, None, :]
    first = vectors[..., :half_dim]
    second = vectors[..., half_dim:]
    return jnp.concatenate(
        [first * cosine - second * sine, second * cosine + first * sine], axis=-1
    )


def regroup(query_part, key_part, value_part, output_part, gate_part, up_part, down_part):
    columns = (
        lax.all_to_all(query_part, "fsdp", split_axis=0, concat_axis=1, tiled=True),
        lax.all_to_all(key_part, "fsdp", split_axis=0, concat_axis=1, tiled=True),
        lax.all_to_all(value_part, "fsdp", split_axis=0, concat_axis=1, tiled=True),
        lax.all_to_all(gate_part, "fsdp", split_axis=0, concat_axis=1, tiled=True),
        lax.all_to_all(up_part, "fsdp", split_axis=0, concat_axis=1, tiled=True),
    )
    rowwise = (
        lax.all_to_all(output_part, "fsdp", split_axis=1, concat_axis=0, tiled=True),
        lax.all_to_all(down_part, "fsdp", split_axis=1, concat_axis=0, tiled=True),
    )
    return (columns[0], columns[1], columns[2], rowwise[0], columns[3], columns[4], rowwise[1])


def attend(query, key_new, value_new, key_cache, value_cache, lengths):
    count_seq = query.shape[0]
    kv_count = query.shape[1]
    head_dim = query.shape[3]
    cache_len = key_cache.shape[1]
    keys = key_cache.reshape(count_seq, cache_len, kv_count, head_dim)
    values = value_cache.reshape(count_seq, cache_len, kv_count, head_dim)
    scale = head_dim ** (-0.5)
    scores = jnp.einsum("bkgd,bjkd->bkgj", query, keys, preferred_element_type=jnp.float32) * scale
    own = (
        jnp.sum(query.astype(jnp.float32) * key_new.astype(jnp.float32)[:, :, None, :], axis=-1)
        * scale
    )
    valid = (lax.broadcasted_iota(jnp.int32, (count_seq, cache_len), 1) < lengths[:, None])[
        :, None, None, :
    ]
    top = jnp.maximum(jnp.max(jnp.where(valid, scores, -1e30), axis=-1), own)
    weights = jnp.where(valid, jnp.exp(scores - top[..., None]), 0.0)
    own_weight = jnp.exp(own - top)
    total = jnp.sum(weights, axis=-1) + own_weight
    probs = (weights / total[..., None]).astype(jnp.bfloat16)
    own_prob = (own_weight / total).astype(jnp.bfloat16)
    mixed = jnp.einsum("bkgj,bjkd->bkgd", probs, values, preferred_element_type=jnp.float32)
    mixed = (
        mixed
        + own_prob.astype(jnp.float32)[..., None] * value_new.astype(jnp.float32)[:, :, None, :]
    )
    return mixed.astype(jnp.bfloat16).reshape(count_seq, -1)


def per_device(
    hidden,
    query_weight,
    key_weight,
    value_weight,
    output_weight,
    gate_weight,
    up_weight,
    down_weight,
    history,
    slot,
    lengths,
    key_cache,
    value_cache,
):
    trainer = (
        query_weight,
        key_weight,
        value_weight,
        output_weight,
        gate_weight,
        up_weight,
        down_weight,
    )
    peaks = jnp.stack([lax.pmax(largest(tensor), ("fsdp", "tp")) for tensor in trainer])
    factors, new_history = scaling(peaks, history, slot)
    arrived = regroup(
        query_weight, key_weight, value_weight, output_weight, gate_weight, up_weight, down_weight
    )
    rollout = tuple((quantize(arrived[number], factors[number]) for number in range(7)))
    (
        query_rollout,
        key_rollout,
        value_rollout,
        output_rollout,
        gate_rollout,
        up_rollout,
        down_rollout,
    ) = rollout
    widened = hidden.astype(jnp.float32)
    squares = jnp.sum(widened * widened, axis=1)
    joined = jnp.concatenate([query_rollout, key_rollout, value_rollout], axis=1)
    partial_value = jnp.dot(hidden, joined, preferred_element_type=jnp.float32)
    summed, total_sq = (
        lax.psum_scatter(partial_value, "fsdp", scatter_dimension=0, tiled=True),
        lax.psum_scatter(squares, "fsdp", scatter_dimension=0, tiled=True),
    )
    inv_rms = lax.rsqrt(total_sq / D + norm_eps)[:, None]
    width_q = query_rollout.shape[1]
    width_k = key_rollout.shape[1]
    query = summed[:, :width_q] * inv_rms / factors[0]
    key_new = summed[:, width_q : width_q + width_k] * inv_rms / factors[1]
    value_new = summed[:, width_q + width_k :] * inv_rms / factors[2]
    count_seq = summed.shape[0]
    query = rotate(query.reshape(count_seq, -1, HEAD_DIM), lengths).astype(jnp.bfloat16)
    query = query.reshape(count_seq, -1, HEADS // KV_HEADS, HEAD_DIM)
    key_new = rotate(key_new.reshape(count_seq, -1, HEAD_DIM), lengths).astype(jnp.bfloat16)
    value_new = value_new.reshape(count_seq, -1, HEAD_DIM).astype(jnp.bfloat16)
    attention_out = attend(query, key_new, value_new, key_cache, value_cache, lengths)
    return (
        attention_out,
        query_rollout,
        key_rollout,
        value_rollout,
        output_rollout,
        gate_rollout,
        up_rollout,
        down_rollout,
        new_history,
    )


def solution(mesh):
    return jax.shard_map(
        per_device,
        mesh=mesh,
        in_specs=(
            P(None, "fsdp"),
            P(None, ("tp", "fsdp")),
            P(None, ("tp", "fsdp")),
            P(None, ("tp", "fsdp")),
            P(("tp", "fsdp"), None),
            P(None, ("tp", "fsdp")),
            P(None, ("tp", "fsdp")),
            P(("tp", "fsdp"), None),
            P(),
            P(),
            P("fsdp"),
            P("fsdp", None, "tp"),
            P("fsdp", None, "tp"),
        ),
        out_specs=(
            P("fsdp", "tp"),
            P("fsdp", "tp"),
            P("fsdp", "tp"),
            P("fsdp", "tp"),
            P("tp", "fsdp"),
            P("fsdp", "tp"),
            P("fsdp", "tp"),
            P("tp", "fsdp"),
            P(),
        ),
        check_vma=False,
    )
```

profile of v0, /device:TPU:0, one launch (start us, length us, event | category | flops | bytes accessed | tf_op | source)
XLA Modules:
  0.0 1055.7 jit_solution(7451371705270785353)
XLA Ops:
  9.3 7.4 all-to-all-start.1
  18.9 10.0 all-to-all-done.1
  38.2 7.1 all-to-all-done.2
  45.3 4.4 all-to-all-start
  54.8 33.7 %all-to-all-done = bf16[16,320,160]{1,2,0:T(8,128)(2,1)} async-done(((bf16[16,320,160]{1,2,0:T(8,128)(2,1)}), bf16[16,320,160]{1,2,0:T(8,128)(2,1)}, u32[]{:S(2)}, u32[]{:S(2)}) %all-to-all-start) | async-done | bytes 1638432 | tf_op jit(solution)/shard_map/all_to_all | solution.py:45
  88.4 10.7 %all-to-all-start.3 = ((bf16[160,16,320]{2,0,1:T(8,128)(2,1)}), bf16[160,16,320]{2,0,1:T(8,128)(2,1)S(1)}, u32[]{:S(2)}, u32[]{:S(2)}) async-start(bf16[160,16,320]{2,0,1:T(8,128)(2,1)} %copy.77), calls=%async_computation.3 | async-start | bytes 3932160 | tf_op jit(solution)/shard_map/all_to_all | solution.py:52
  99.1 12.7 %copy.78 = bf16[5120,864]{1,0:T(8,128)(2,1)} copy(bf16[5120,864]{0,1:T(8,128)(2,1)} %param.18) | data formatting | bytes 17694720 | tf_op args[5]
  111.8 26.0 %all-to-all-done.3 = bf16[160,16,320]{2,0,1:T(8,128)(2,1)S(1)} async-done(((bf16[160,16,320]{2,0,1:T(8,128)(2,1)}), bf16[160,16,320]{2,0,1:T(8,128)(2,1)S(1)}, u32[]{:S(2)}, u32[]{:S(2)}) %all-to-all-start.3) | async-done | bytes 1638432 | tf_op jit(solution)/shard_map/all_to_all | solution.py:52
  139.1 10.7 %all-to-all-start.4 = ((bf16[16,320,864]{2,1,0:T(8,128)(2,1)}), bf16[16,320,864]{2,1,0:T(8,128)(2,1)}, u32[]{:S(2)}, u32[]{:S(2)}) async-start(bf16[16,320,864]{2,1,0:T(8,128)(2,1)} %bitcast.74), calls=%async_computation.4 | async-start | bytes 18350080 | tf_op jit(solution)/shard_map/all_to_all | solution.py:48
  149.8 12.7 %copy.80 = bf16[5120,864]{1,0:T(8,128)(2,1)} copy(bf16[5120,864]{0,1:T(8,128)(2,1)} %param.19) | data formatting | bytes 17694720 | tf_op args[6]
  162.5 151.6 %all-to-all-done.4 = bf16[16,320,864]{2,1,0:T(8,128)(2,1)} async-done(((bf16[16,320,864]{2,1,0:T(8,128)(2,1)}), bf16[16,320,864]{2,1,0:T(8,128)(2,1)}, u32[]{:S(2)}, u32[]{:S(2)}) %all-to-all-start.4) | async-done | bytes 8847392 | tf_op jit(solution)/shard_map/all_to_all | solution.py:48
  314.1 39.7 %all-to-all-start.5 = ((bf16[16,320,864]{2,1,0:T(8,128)(2,1)}), bf16[16,320,864]{2,1,0:T(8,128)(2,1)}, u32[]{:S(2)}, u32[]{:S(2)}) async-start(bf16[16,320,864]{2,1,0:T(8,128)(2,1)} %bitcast.75), calls=%async_computation.5 | async-start | bytes 18350080 | tf_op jit(solution)/shard_map/all_to_all | solution.py:49
  353.8 12.7 %copy.82 = bf16[864,5120]{0,1:T(8,128)(2,1)} copy(bf16[864,5120]{1,0:T(8,128)(2,1)} %param.20) | data formatting | bytes 17694720 | tf_op args[7]
  366.5 151.6 %all-to-all-done.5 = bf16[16,320,864]{2,1,0:T(8,128)(2,1)} async-done(((bf16[16,320,864]{2,1,0:T(8,128)(2,1)}), bf16[16,320,864]{2,1,0:T(8,128)(2,1)}, u32[]{:S(2)}, u32[]{:S(2)}) %all-to-all-start.5) | async-done | bytes 8847392 | tf_op jit(solution)/shard_map/all_to_all | solution.py:49
  518.1 40.0 %all-to-all-start.6 = ((bf16[864,16,320]{0,2,1:T(8,128)(2,1)}), bf16[864,16,320]{0,2,1:T(8,128)(2,1)}, u32[]{:S(2)}, u32[]{:S(2)}) async-start(bf16[864,16,320]{0,2,1:T(8,128)(2,1)} %bitcast.73), calls=%async_computation.6 | async-start | bytes 18350080 | tf_op jit(solution)/shard_map/all_to_all | solution.py:53
  563.3 5.9 abs_reduce_fusion.2
  569.3 5.8 abs_reduce_fusion.1
  577.4 201.6 %all-reduce.2 = (f32[1]{0:T(128)}, f32[1]{0:T(128)}, f32[1]{0:T(128)}, f32[1]{0:T(128)}, f32[1]{0:T(128)}, /*index=5*/f32[1]{0:T(128)}, f32[1]{0:T(128)}) all-reduce(f32[1]{0:T(128)} %bitcast, f32[1]{0:T(128)} %bitcast.1, f32[1]{0:T(128)} %bitcast.2, f32[1]{0:T(128)} %bitcast.3, ...), channel_id=1, replica_groups=mesh['fsdp'=16,'tp'=2] {'fsdp','tp'}, use_global_device_ids=true, to_apply=%region_1.0 | all-reduce | flops 7 | bytes 56 | tf_op jit(solution)/shard_map/pmax | solution.py:112
  781.0 4.5 stack.31
  785.7 31.4 %all-reduce.1 = f32[32]{0:T(128)S(1)} all-reduce(f32[32]{0:T(128)S(1)} %multiply_reduce_fusion), channel_id=3, replica_groups=mesh['fsdp'=16,'tp'=2] {'fsdp'}, use_global_device_ids=true, to_apply=%region_17.18.clone | all-reduce | flops 32 | bytes 256
  835.9 81.5 %all-reduce.5.cloned.1.call-done = f32[32,3584]{1,0:T(8,128)} async-done(((f32[32,3584]{1,0:T(8,128)}), f32[32,3584]{1,0:T(8,128)}) %all-reduce.5.cloned.1.call-update) | async-done | bytes 458768
  921.6 5.8 select_reduce_fusion
  927.9 4.7 fusion.20
  933.3 9.7 fusion
  943.0 12.4 %copy.79 = bf16[320,16,864]{2,1,0:T(8,128)(2,1)} copy(bf16[320,16,864]{2,0,1:T(8,128)(2,1)} %fusion) | data formatting | bytes 17694720 | tf_op jit(solution)/shard_map/convert_element_type | solution.py:26
  955.4 16.3 %convert_element_type.218 = bf16[320,13824]{1,0:T(8,128)(2,1)} reshape(bf16[320,16,864]{2,1,0:T(8,128)(2,1)} %copy.79) | data formatting | bytes 17694720 | tf_op jit(solution)/shard_map/convert_element_type | solution.py:26
  971.7 9.8 fusion.1
  981.5 12.4 %copy.81 = bf16[320,16,864]{2,1,0:T(8,128)(2,1)} copy(bf16[320,16,864]{2,0,1:T(8,128)(2,1)} %fusion.1) | data formatting | bytes 17694720 | tf_op jit(solution)/shard_map/convert_element_type | solution.py:26
  993.9 16.3 %convert_element_type.222 = bf16[320,13824]{1,0:T(8,128)(2,1)} reshape(bf16[320,16,864]{2,1,0:T(8,128)(2,1)} %copy.81) | data formatting | bytes 17694720 | tf_op jit(solution)/shard_map/convert_element_type | solution.py:26
  1010.3 9.8 fusion.2
  1020.1 12.4 %copy.83 = bf16[16,864,320]{1,0,2:T(8,128)(2,1)} copy(bf16[16,864,320]{1,2,0:T(8,128)(2,1)} %fusion.2) | data formatting | bytes 17694720 | tf_op jit(solution)/shard_map/convert_element_type | solution.py:26
  1032.4 16.1 %convert_element_type.226 = bf16[13824,320]{0,1:T(8,128)(2,1)} reshape(bf16[16,864,320]{1,0,2:T(8,128)(2,1)} %copy.83) | data formatting | bytes 17694720 | tf_op jit(solution)/shard_map/convert_element_type | solution.py:26
  (83 shorter events, 52.2 us)
Async XLA Ops:
  9.3 19.6 %all-to-all-start.1 = ((bf16[16,320,32]{1,2,0:T(8,128)(2,1)}), bf16[16,320,32]{1,2,0:T(8,128)(2,1)S(1)}, u32[]{:S(2)}, u32[]{:S(2)}) async-start(bf16[16,320,32]{1,2,0:T(8,128)(2,1)} %copy.69), calls=%async_computation.1 | async-start | bytes 786432 | tf_op jit(solution)/shard_map/all_to_all | solution.py:46
  28.9 0.7 copy-start.3
  29.6 15.7 %all-to-all-start.2 = ((bf16[16,320,32]{1,2,0:T(8,128)(2,1)}), bf16[16,320,32]{1,2,0:T(8,128)(2,1)S(1)}, u32[]{:S(2)}, u32[]{:S(2)}) async-start(bf16[16,320,32]{1,2,0:T(8,128)(2,1)} %copy.70), calls=%async_computation.2 | async-start | bytes 786432 | tf_op jit(solution)/shard_map/all_to_all | solution.py:47
  45.3 66.5 %copy-start.5 = (bf16[16,320,32]{1,2,0:T(8,128)(2,1)}, bf16[16,320,32]{1,2,0:T(8,128)(2,1)S(1)}, u32[]{:S(2)}) copy-start(bf16[16,320,32]{1,2,0:T(8,128)(2,1)S(1)} %all-to-all-done.2) | copy-start | bytes 983044
  45.3 43.1 %all-to-all-start = ((bf16[16,320,160]{1,2,0:T(8,128)(2,1)}), bf16[16,320,160]{1,2,0:T(8,128)(2,1)}, u32[]{:S(2)}, u32[]{:S(2)}) async-start(bf16[16,320,160]{1,2,0:T(8,128)(2,1)} %copy.68), calls=%async_computation | async-start | bytes 3932160 | tf_op jit(solution)/shard_map/all_to_all | solution.py:45
  88.4 49.4 %all-to-all-start.3 = ((bf16[160,16,320]{2,0,1:T(8,128)(2,1)}), bf16[160,16,320]{2,0,1:T(8,128)(2,1)S(1)}, u32[]{:S(2)}, u32[]{:S(2)}) async-start(bf16[160,16,320]{2,0,1:T(8,128)(2,1)} %copy.77), calls=%async_computation.3 | async-start | bytes 3932160 | tf_op jit(solution)/shard_map/all_to_all | solution.py:52
  137.8 1.3 copy-start
  139.1 175.0 %all-to-all-start.4 = ((bf16[16,320,864]{2,1,0:T(8,128)(2,1)}), bf16[16,320,864]{2,1,0:T(8,128)(2,1)}, u32[]{:S(2)}, u32[]{:S(2)}) async-start(bf16[16,320,864]{2,1,0:T(8,128)(2,1)} %bitcast.74), calls=%async_computation.4 | async-start | bytes 18350080 | tf_op jit(solution)/shard_map/all_to_all | solution.py:48
  314.1 204.0 %all-to-all-start.5 = ((bf16[16,320,864]{2,1,0:T(8,128)(2,1)}), bf16[16,320,864]{2,1,0:T(8,128)(2,1)}, u32[]{:S(2)}, u32[]{:S(2)}) async-start(bf16[16,320,864]{2,1,0:T(8,128)(2,1)} %bitcast.75), calls=%async_computation.5 | async-start | bytes 18350080 | tf_op jit(solution)/shard_map/all_to_all | solution.py:49
  518.1 43.6 %copy-start.1 = (bf16[5120,160]{0,1:T(8,128)(2,1)S(1)}, bf16[5120,160]{0,1:T(8,128)(2,1)}, u32[]{:S(2)}) copy-start(bf16[5120,160]{0,1:T(8,128)(2,1)} %param.14) | copy-start | bytes 4915204
  518.1 44.4 %copy-start.2 = (bf16[160,5120]{1,0:T(8,128)(2,1)S(1)}, bf16[160,5120]{1,0:T(8,128)(2,1)}, u32[]{:S(2)}) copy-start(bf16[160,5120]{1,0:T(8,128)(2,1)} %param.17) | copy-start | bytes 4915204
  518.1 492.2 %all-to-all-start.6 = ((bf16[864,16,320]{0,2,1:T(8,128)(2,1)}), bf16[864,16,320]{0,2,1:T(8,128)(2,1)}, u32[]{:S(2)}, u32[]{:S(2)}) async-start(bf16[864,16,320]{0,2,1:T(8,128)(2,1)} %bitcast.73), calls=%async_computation.6 | async-start | bytes 18350080 | tf_op jit(solution)/shard_map/all_to_all | solution.py:53
  558.1 359.4 %all-reduce.5.cloned.1.call-start = ((), (), s32[]{:S(2)}) async-start(), calls=%async_computation.7 | async-start | bytes 917504
  563.3 11.8 %slice-start = ((s8[8847360]{0:T(1024)(128)(4,1)}), s8[4194304]{0:T(1024)(128)(4,1)S(1)}, s32[]{:S(2)}) async-start(s8[8847360]{0:T(1024)(128)(4,1)} %bitcast.76), calls=%async_computation.8 | async-start | bytes 8388608
  563.3 11.8 %slice-start.1 = ((s8[8847360]{0:T(1024)(128)(4,1)}), s8[4194304]{0:T(1024)(128)(4,1)S(1)}, s32[]{:S(2)}) async-start(s8[8847360]{0:T(1024)(128)(4,1)} %bitcast.76), calls=%async_computation.9 | async-start | bytes 8388608
  569.2 5.9 slice-start.2
  569.2 210.5 %copy-start.9 = (s32[2]{0:T(128)S(1)}, s32[2]{0:T(128)}, u32[]{:S(2)}) copy-start(s32[2]{0:T(128)} %param.23) | copy-start | bytes 28
  569.2 210.5 %copy-start.10 = (u32[32]{0:T(128)S(1)}, u32[32]{0:T(128)}, u32[]{:S(2)}) copy-start(u32[32]{0:T(128)} %constant.29) | copy-start | bytes 388
  569.2 216.3 %copy-start.8 = (bf16[32,320]{1,0:T(8,128)(2,1)S(1)}, bf16[32,320]{1,0:T(8,128)(2,1)}, u32[]{:S(2)}) copy-start(bf16[32,320]{1,0:T(8,128)(2,1)} %param.13) | copy-start | bytes 61444
  569.2 247.9 %copy-start.7 = (f32[7,1024]{1,0:T(8,128)S(1)}, f32[7,1024]{1,0:T(8,128)}, u32[]{:S(2)}) copy-start(f32[7,1024]{1,0:T(8,128)} %param.21) | copy-start | bytes 86020
  569.2 249.6 %copy-start.4 = (bf16[16,320,32]{1,2,0:T(8,128)(2,1)S(1)}, bf16[16,320,32]{1,2,0:T(8,128)(2,1)}, u32[]{:S(2)}) copy-start(bf16[16,320,32]{1,2,0:T(8,128)(2,1)} %copy-done.3) | copy-start | bytes 983044
  569.3 251.2 %copy-start.6 = (bf16[16,320,32]{1,2,0:T(8,128)(2,1)S(1)}, bf16[16,320,32]{1,2,0:T(8,128)(2,1)}, u32[]{:S(2)}) copy-start(bf16[16,320,32]{1,2,0:T(8,128)(2,1)} %copy-done.5) | copy-start | bytes 983044
Sparse Core Ops, SparseCore 0:
  829.7 87.6 all-reduce.4
where the time goes:
time: 1060 us
  waiting for transfers between devices  461 us (43%)
  blocking collectives  233 us (22%)
  local copies, waits for them, and re-layouts  156 us (15%)
  starting transfers between devices  117 us (11%)
  other arithmetic  60.6 us (6%)
  between operations  15.9 us (2%)
  matrix products  12.2 us (1%)
    pmax x1, blocking collectives, per_device(): lax.pmax(largest(tensor), ('fsdp', 'tp'))  202 us
    all_to_all x1, waiting for transfers between devices, regroup(): lax.all_to_all(gate_part, 'fsdp', split_axis=0, concat_axis=1, tiled=True)  152 us
    all_to_all x1, waiting for transfers between devices, regroup(): lax.all_to_all(up_part, 'fsdp', split_axis=0, concat_axis=1, tiled=True)  152 us
    convert_element_type x6, local copies, waits for them, and re-layouts, quantize(): return (tensor.astype(jnp.float32) * factor).astype(jnp.bfloat16)  86 us
    unnamed x2, waiting for transfers between devices  81.5 us
    unnamed x36, local copies, waits for them, and re-layouts  49.6 us
    all_to_all x1, starting transfers between devices, regroup(): lax.all_to_all(down_part, 'fsdp', split_axis=1, concat_axis=0, tiled=True)  40 us
    all_to_all x1, starting transfers between devices, regroup(): lax.all_to_all(up_part, 'fsdp', split_axis=0, concat_axis=1, tiled=True)  39.7 us
  transfers between devices with their start and end apart: 8, of which 7 were waited for; matrix products, arithmetic and copies ran while one was open for 17% of the time, Pallas kernels for 0%

commit v1 on v0

--- a/solution.py
+++ b/solution.py
@@ -45,7 +45,12 @@
         lax.all_to_all(query_part, "fsdp", split_axis=0, concat_axis=1, tiled=True),
         lax.all_to_all(key_part, "fsdp", split_axis=0, concat_axis=1, tiled=True),
         lax.all_to_all(value_part, "fsdp", split_axis=0, concat_axis=1, tiled=True),
-        lax.all_to_all(gate_part, "fsdp", split_axis=0, concat_axis=1, tiled=True),
+        jnp.concatenate(
+            lax.all_to_all(
+                jnp.stack(jnp.split(gate_part, lax.axis_size("fsdp"), axis=0)), "fsdp", 0, 0
+            ),
+            axis=1,
+        ),
         lax.all_to_all(up_part, "fsdp", split_axis=0, concat_axis=1, tiled=True),
     )
     rowwise = (

time: 1060 us -> 1070 us (level)
  local copies, waits for them, and re-layouts: 156 us -> 208 us
  waiting for transfers between devices: 461 us -> 416 us
    unnamed x36 -> x74, local copies, waits for them, and re-layouts: 49.6 us -> 92.4 us
    all_to_all x1, waiting for transfers between devices: 26 us -> 0.01 us  [regroup(): lax.all_to_all(output_part, 'fsdp', split_axis=1, concat_axis=0, tiled=True)]
    all_to_all x1, waiting for transfers between devices: 33.7 us -> 13.6 us  [regroup(): lax.all_to_all(query_part, 'fsdp', split_axis=0, concat_axis=1, tiled=True)]
  transfers between devices with their start and end apart: 8 -> 8, of which waited for: 7 -> 6; matrix products, arithmetic and copies ran while one was open for 17% -> 22% of each run, Pallas kernels for 0% -> 0%
where the time goes in v1:
time: 1070 us; the launch traced here: 1060 us
  waiting for transfers between devices  416 us (39%)
  blocking collectives  233 us (22%)
  local copies, waits for them, and re-layouts  208 us (19%)
  starting transfers between devices  112 us (10%)
  other arithmetic  60.3 us (6%)
  between operations  15.8 us (1%)
  matrix products  12.2 us (1%)
    pmax x1, blocking collectives, per_device(): lax.pmax(largest(tensor), ('fsdp', 'tp'))  202 us
    all_to_all x1, waiting for transfers between devices, regroup(): lax.all_to_all(jnp.stack(jnp.split(gate_part, lax.axis_size('fsdp'), axis...  152 us
    all_to_all x1, waiting for transfers between devices, regroup(): lax.all_to_all(up_part, 'fsdp', split_axis=0, concat_axis=1, tiled=True)  151 us
    unnamed x74, local copies, waits for them, and re-layouts  92.4 us
    convert_element_type x6, local copies, waits for them, and re-layouts, quantize(): return (tensor.astype(jnp.float32) * factor).astype(jnp.bfloat16)  86.2 us
    unnamed x2, waiting for transfers between devices  81.8 us
    all_to_all x1, starting transfers between devices, regroup(): lax.all_to_all(down_part, 'fsdp', split_axis=1, concat_axis=0, tiled=True)  40 us
    all_to_all x1, starting transfers between devices, regroup(): lax.all_to_all(up_part, 'fsdp', split_axis=0, concat_axis=1, tiled=True)  39.9 us
  transfers between devices with their start and end apart: 8, of which 6 were waited for; matrix products, arithmetic and copies ran while one was open for 22% of the time, Pallas kernels for 0%

profile of v1, /device:TPU:0, one launch (start us, length us, event | category | flops | bytes accessed | tf_op | source)
XLA Modules:
  0.0 1056.9 jit_solution(5502298691678608252)
XLA Ops:
  9.3 7.4 all-to-all-start.1
  18.9 10.0 all-to-all-done.1
  29.7 3.6 all-to-all-start.2
  38.2 7.1 all-to-all-done.2
  46.1 4.4 all-to-all-start
  50.5 7.8 fusion.40
  75.7 13.6 %all-to-all-done = bf16[16,320,160]{1,2,0:T(8,128)(2,1)} async-done(((bf16[16,320,160]{1,2,0:T(8,128)(2,1)}), bf16[16,320,160]{1,2,0:T(8,128)(2,1)}, u32[]{:S(2)}, u32[]{:S(2)}) %all-to-all-start) | async-done | bytes 1638432 | tf_op jit(solution)/shard_map/all_to_all | solution.py:45
  89.2 10.7 %all-to-all-start.3 = ((bf16[160,16,320]{2,0,1:T(8,128)(2,1)}), bf16[160,16,320]{2,0,1:T(8,128)(2,1)S(1)}, u32[]{:S(2)}, u32[]{:S(2)}) async-start(bf16[160,16,320]{2,0,1:T(8,128)(2,1)} %copy.110), calls=%async_computation.3 | async-start | bytes 3932160 | tf_op jit(solution)/shard_map/all_to_all | solution.py:57
  144.8 6.1 all-to-all-start.4
  150.8 12.7 %copy.128 = bf16[5120,864]{1,0:T(8,128)(2,1)} copy(bf16[5120,864]{0,1:T(8,128)(2,1)} %param.19) | data formatting | bytes 17694720 | tf_op args[6]
  163.6 151.5 %all-to-all-done.4 = bf16[16,320,864]{2,1,0:T(8,128)(2,1)} async-done(((bf16[16,320,864]{2,1,0:T(8,128)(2,1)}), bf16[16,320,864]{2,1,0:T(8,128)(2,1)}, u32[]{:S(2)}, u32[]{:S(2)}) %all-to-all-start.4) | async-done | bytes 8847392 | tf_op jit(solution)/shard_map/all_to_all | solution.py:49
  315.1 39.9 %all-to-all-start.5 = ((bf16[16,320,864]{2,1,0:T(8,128)(2,1)}), bf16[16,320,864]{2,1,0:T(8,128)(2,1)}, u32[]{:S(2)}, u32[]{:S(2)}) async-start(bf16[16,320,864]{2,1,0:T(8,128)(2,1)} %bitcast.105), calls=%async_computation.5 | async-start | bytes 18350080 | tf_op jit(solution)/shard_map/all_to_all | solution.py:54
  355.0 12.8 %copy.130 = bf16[864,5120]{0,1:T(8,128)(2,1)} copy(bf16[864,5120]{1,0:T(8,128)(2,1)} %param.20) | data formatting | bytes 17694720 | tf_op args[7]
  367.8 151.5 %all-to-all-done.5 = bf16[16,320,864]{2,1,0:T(8,128)(2,1)} async-done(((bf16[16,320,864]{2,1,0:T(8,128)(2,1)}), bf16[16,320,864]{2,1,0:T(8,128)(2,1)}, u32[]{:S(2)}, u32[]{:S(2)}) %all-to-all-start.5) | async-done | bytes 8847392 | tf_op jit(solution)/shard_map/all_to_all | solution.py:54
  519.3 40.0 %all-to-all-start.6 = ((bf16[864,16,320]{0,2,1:T(8,128)(2,1)}), bf16[864,16,320]{0,2,1:T(8,128)(2,1)}, u32[]{:S(2)}, u32[]{:S(2)}) async-start(bf16[864,16,320]{0,2,1:T(8,128)(2,1)} %bitcast.104), calls=%async_computation.6 | async-start | bytes 18350080 | tf_op jit(solution)/shard_map/all_to_all | solution.py:58
  564.2 5.9 abs_reduce_fusion.2
  570.1 5.9 abs_reduce_fusion.1
  578.2 202.0 %all-reduce.2 = (f32[1]{0:T(128)}, f32[1]{0:T(128)}, f32[1]{0:T(128)}, f32[1]{0:T(128)}, f32[1]{0:T(128)}, /*index=5*/f32[1]{0:T(128)}, f32[1]{0:T(128)}) all-reduce(f32[1]{0:T(128)} %bitcast, f32[1]{0:T(128)} %bitcast.1, f32[1]{0:T(128)} %bitcast.2, f32[1]{0:T(128)} %bitcast.3, ...), channel_id=1, replica_groups=mesh['fsdp'=16,'tp'=2] {'fsdp','tp'}, use_global_device_ids=true, to_apply=%region_1.0 | all-reduce | flops 7 | bytes 56 | tf_op jit(solution)/shard_map/pmax | solution.py:117
  782.2 4.6 stack.82
  786.9 31.4 %all-reduce.1 = f32[32]{0:T(128)S(1)} all-reduce(f32[32]{0:T(128)S(1)} %multiply_reduce_fusion), channel_id=3, replica_groups=mesh['fsdp'=16,'tp'=2] {'fsdp'}, use_global_device_ids=true, to_apply=%region_17.18.clone | all-reduce | flops 32 | bytes 256
  836.8 81.8 %all-reduce.5.cloned.1.call-done = f32[32,3584]{1,0:T(8,128)} async-done(((f32[32,3584]{1,0:T(8,128)}), f32[32,3584]{1,0:T(8,128)}) %all-reduce.5.cloned.1.call-update) | async-done | bytes 458768
  922.7 5.8 select_reduce_fusion
  928.9 4.7 fusion.20
  934.3 9.7 fusion
  944.0 12.4 %copy.127 = bf16[320,16,864]{2,1,0:T(8,128)(2,1)} copy(bf16[320,16,864]{2,0,1:T(8,128)(2,1)} %fusion) | data formatting | bytes 17694720 | tf_op jit(solution)/shard_map/convert_element_type | solution.py:26
  956.4 16.5 %convert_element_type.218 = bf16[320,13824]{1,0:T(8,128)(2,1)} reshape(bf16[320,16,864]{2,1,0:T(8,128)(2,1)} %copy.127) | data formatting | bytes 17694720 | tf_op jit(solution)/shard_map/convert_element_type | solution.py:26
  973.0 9.7 fusion.1
  982.7 12.5 %copy.129 = bf16[320,16,864]{2,1,0:T(8,128)(2,1)} copy(bf16[320,16,864]{2,0,1:T(8,128)(2,1)} %fusion.1) | data formatting | bytes 17694720 | tf_op jit(solution)/shard_map/convert_element_type | solution.py:26
  995.2 16.3 %convert_element_type.222 = bf16[320,13824]{1,0:T(8,128)(2,1)} reshape(bf16[320,16,864]{2,1,0:T(8,128)(2,1)} %copy.129) | data formatting | bytes 17694720 | tf_op jit(solution)/shard_map/convert_element_type | solution.py:26
  1011.5 9.9 fusion.2
  1021.3 12.4 %copy.131 = bf16[16,864,320]{1,0,2:T(8,128)(2,1)} copy(bf16[16,864,320]{1,2,0:T(8,128)(2,1)} %fusion.2) | data formatting | bytes 17694720 | tf_op jit(solution)/shard_map/convert_element_type | solution.py:26
  1033.7 16.1 %convert_element_type.226 = bf16[13824,320]{0,1:T(8,128)(2,1)} reshape(bf16[16,864,320]{1,0,2:T(8,128)(2,1)} %copy.131) | data formatting | bytes 17694720 | tf_op jit(solution)/shard_map/convert_element_type | solution.py:26
  (123 shorter events, 104.4 us)
Async XLA Ops:
  9.3 19.6 %all-to-all-start.1 = ((bf16[16,320,32]{1,2,0:T(8,128)(2,1)}), bf16[16,320,32]{1,2,0:T(8,128)(2,1)S(1)}, u32[]{:S(2)}, u32[]{:S(2)}) async-start(bf16[16,320,32]{1,2,0:T(8,128)(2,1)} %copy.102), calls=%async_computation.1 | async-start | bytes 786432 | tf_op jit(solution)/shard_map/all_to_all | solution.py:46
  28.9 0.8 copy-start.7
  29.7 15.7 %all-to-all-start.2 = ((bf16[16,320,32]{1,2,0:T(8,128)(2,1)}), bf16[16,320,32]{1,2,0:T(8,128)(2,1)S(1)}, u32[]{:S(2)}, u32[]{:S(2)}) async-start(bf16[16,320,32]{1,2,0:T(8,128)(2,1)} %copy.103), calls=%async_computation.2 | async-start | bytes 786432 | tf_op jit(solution)/shard_map/all_to_all | solution.py:47
  45.4 0.7 copy-start.9
  46.1 43.1 %all-to-all-start = ((bf16[16,320,160]{1,2,0:T(8,128)(2,1)}), bf16[16,320,160]{1,2,0:T(8,128)(2,1)}, u32[]{:S(2)}, u32[]{:S(2)}) async-start(bf16[16,320,160]{1,2,0:T(8,128)(2,1)} %copy.101), calls=%async_computation | async-start | bytes 3932160 | tf_op jit(solution)/shard_map/all_to_all | solution.py:45
  89.2 55.5 %all-to-all-start.3 = ((bf16[160,16,320]{2,0,1:T(8,128)(2,1)}), bf16[160,16,320]{2,0,1:T(8,128)(2,1)S(1)}, u32[]{:S(2)}, u32[]{:S(2)}) async-start(bf16[160,16,320]{2,0,1:T(8,128)(2,1)} %copy.110), calls=%async_computation.3 | async-start | bytes 3932160 | tf_op jit(solution)/shard_map/all_to_all | solution.py:57
  124.6 18.4 %copy-start.3 = (bf16[320,864]{1,0:T(8,128)(2,1)S(1)}, bf16[320,864]{1,0:T(8,128)(2,1)}, u32[]{:S(2)}) copy-start(bf16[320,864]{1,0:T(8,128)(2,1)} %copy.150) | copy-start | bytes 1658884
  125.7 15.5 %copy-start.6 = (bf16[320,864]{1,0:T(8,128)(2,1)S(1)}, bf16[320,864]{1,0:T(8,128)(2,1)}, u32[]{:S(2)}) copy-start(bf16[320,864]{1,0:T(8,128)(2,1)} %copy.148) | copy-start | bytes 1658884
  125.7 16.4 %copy-start.5 = (bf16[320,864]{1,0:T(8,128)(2,1)S(1)}, bf16[320,864]{1,0:T(8,128)(2,1)}, u32[]{:S(2)}) copy-start(bf16[320,864]{1,0:T(8,128)(2,1)} %copy.149) | copy-start | bytes 1658884
  125.7 18.2 %copy-start.4 = (bf16[320,864]{1,0:T(8,128)(2,1)S(1)}, bf16[320,864]{1,0:T(8,128)(2,1)}, u32[]{:S(2)}) copy-start(bf16[320,864]{1,0:T(8,128)(2,1)} %copy.151) | copy-start | bytes 1658884
  144.8 18.8 %copy-start = (bf16[160,16,320]{2,0,1:T(8,128)(2,1)}, bf16[160,16,320]{2,0,1:T(8,128)(2,1)S(1)}, u32[]{:S(2)}) copy-start(bf16[160,16,320]{2,0,1:T(8,128)(2,1)S(1)} %all-to-all-done.3) | copy-start | bytes 4915204
  144.8 170.3 %all-to-all-start.4 = ((bf16[16,320,864]{2,1,0:T(8,128)(2,1)}), bf16[16,320,864]{2,1,0:T(8,128)(2,1)}, u32[]{:S(2)}, u32[]{:S(2)}) async-start(bf16[16,320,864]{2,1,0:T(8,128)(2,1)} %bitcast_dynamic-update-slice_fusion), calls=%async_computation.4 | async-start | bytes 18350080 | tf_op jit(solution)/shard_map/all_to_all | solution.py:49
  315.1 204.2 %all-to-all-start.5 = ((bf16[16,320,864]{2,1,0:T(8,128)(2,1)}), bf16[16,320,864]{2,1,0:T(8,128)(2,1)}, u32[]{:S(2)}, u32[]{:S(2)}) async-start(bf16[16,320,864]{2,1,0:T(8,128)(2,1)} %bitcast.105), calls=%async_computation.5 | async-start | bytes 18350080 | tf_op jit(solution)/shard_map/all_to_all | solution.py:54
  519.3 43.3 %copy-start.1 = (bf16[5120,160]{0,1:T(8,128)(2,1)S(1)}, bf16[5120,160]{0,1:T(8,128)(2,1)}, u32[]{:S(2)}) copy-start(bf16[5120,160]{0,1:T(8,128)(2,1)} %param.14) | copy-start | bytes 4915204
  519.3 44.1 %copy-start.2 = (bf16[160,5120]{1,0:T(8,128)(2,1)S(1)}, bf16[160,5120]{1,0:T(8,128)(2,1)}, u32[]{:S(2)}) copy-start(bf16[160,5120]{1,0:T(8,128)(2,1)} %param.17) | copy-start | bytes 4915204
  519.3 492.2 %all-to-all-start.6 = ((bf16[864,16,320]{0,2,1:T(8,128)(2,1)}), bf16[864,16,320]{0,2,1:T(8,128)(2,1)}, u32[]{:S(2)}, u32[]{:S(2)}) async-start(bf16[864,16,320]{0,2,1:T(8,128)(2,1)} %bitcast.104), calls=%async_computation.6 | async-start | bytes 18350080 | tf_op jit(solution)/shard_map/all_to_all | solution.py:58
  559.2 359.4 %all-reduce.5.cloned.1.call-start = ((), (), s32[]{:S(2)}) async-start(), calls=%async_computation.7 | async-start | bytes 917504
  564.1 11.8 %slice-start = ((s8[8847360]{0:T(1024)(128)(4,1)}), s8[4194304]{0:T(1024)(128)(4,1)S(1)}, s32[]{:S(2)}) async-start(s8[8847360]{0:T(1024)(128)(4,1)} %bitcast.106), calls=%async_computation.8 | async-start | bytes 8388608
  564.1 11.8 %slice-start.1 = ((s8[8847360]{0:T(1024)(128)(4,1)}), s8[4194304]{0:T(1024)(128)(4,1)S(1)}, s32[]{:S(2)}) async-start(s8[8847360]{0:T(1024)(128)(4,1)} %bitcast.106), calls=%async_computation.9 | async-start | bytes 8388608
  570.1 5.9 slice-start.2
  570.1 210.8 %copy-start.13 = (s32[2]{0:T(128)S(1)}, s32[2]{0:T(128)}, u32[]{:S(2)}) copy-start(s32[2]{0:T(128)} %param.23) | copy-start | bytes 28
  570.1 210.8 %copy-start.14 = (u32[32]{0:T(128)S(1)}, u32[32]{0:T(128)}, u32[]{:S(2)}) copy-start(u32[32]{0:T(128)} %constant.29) | copy-start | bytes 388
  570.1 216.7 %copy-start.12 = (bf16[32,320]{1,0:T(8,128)(2,1)S(1)}, bf16[32,320]{1,0:T(8,128)(2,1)}, u32[]{:S(2)}) copy-start(bf16[32,320]{1,0:T(8,128)(2,1)} %param.13) | copy-start | bytes 61444
  570.1 248.3 %copy-start.11 = (f32[7,1024]{1,0:T(8,128)S(1)}, f32[7,1024]{1,0:T(8,128)}, u32[]{:S(2)}) copy-start(f32[7,1024]{1,0:T(8,128)} %param.21) | copy-start | bytes 86020
  570.1 250.0 %copy-start.8 = (bf16[16,320,32]{1,2,0:T(8,128)(2,1)S(1)}, bf16[16,320,32]{1,2,0:T(8,128)(2,1)}, u32[]{:S(2)}) copy-start(bf16[16,320,32]{1,2,0:T(8,128)(2,1)} %copy-done.7) | copy-start | bytes 983044
  570.1 251.6 %copy-start.10 = (bf16[16,320,32]{1,2,0:T(8,128)(2,1)S(1)}, bf16[16,320,32]{1,2,0:T(8,128)(2,1)}, u32[]{:S(2)}) copy-start(bf16[16,320,32]{1,2,0:T(8,128)(2,1)} %copy-done.9) | copy-start | bytes 983044
Sparse Core Ops, SparseCore 0:
  830.8 87.6 all-reduce.4
